TPU v7x, 32 devices: a whole 2x2x4 slice. The times are simulated.
32 devices in a mesh: cell: 16 (over z, y, core), band: 2 (over x).
Axes of the slice: x: 2, y: 2, z: 4, core: 2. Of those that a mesh axis runs over, the one named last changes fastest.
Arguments:
- positions: bfloat16 [32, 3, 96, 192], P('cell', None, 'band'), may hold values from -6 to 6
- densities: bfloat16 [32, 3, 96, 192], P('cell', None, 'band'), may hold values from -6 to 6
- operator: bfloat16 [640, 96, 192], P('cell', 'band'), may hold values from -0.046875 to 0.046875
- target_shift: int32 [32, 16], P('cell'), may hold values from 0 to 191
- weights: float32 [640], replicated, may hold values from 0.02 to 0.2
Outputs:
- velocity: float32 [32, 3, 16], P('cell')
All inputs are finite; a program needn't handle non-finite values.
Results may differ from a plain program's by a relative error of at most 0.0003.
Values may be sent and summed in bfloat16 or wider, within the bound.
A program may use at most 64 MiB of HBM per device.

v0:
```python
import jax
import jax.numpy as jnp
from jax import lax
from jax.sharding import PartitionSpec as P

blob_radius = 0.5


def stokes(target, rows, weights):
    spread = target[:, :, :, None] - rows[:, 0:3]
    force = rows[:, 3:6]
    dist_sq = jnp.sum(spread * spread, axis=1)
    along = jnp.sum(spread * force, axis=1)
    blob_sq = blob_radius * blob_radius
    numer = (dist_sq + 2.0 * blob_sq)[:, None] * force + along[:, None] * spread
    kernel = weights / (dist_sq + blob_sq) ** 1.5
    return jnp.sum(numer * kernel[:, None], axis=-1)


def shifted_rows(source, shifts):
    caps_count, comps, lat_count, lon_count = source.shape
    doubled = jnp.concatenate([source, source], axis=3)
    zero = jnp.int32(0)

    def per_capsule(block, capsule_shifts):

        def per_target(offset):
            return lax.dynamic_slice(block, (zero, zero, offset), (comps, lat_count, lon_count))

        return jax.vmap(per_target)(capsule_shifts)

    rolled = jax.vmap(per_capsule)(doubled, shifts)
    rolled = jnp.transpose(rolled, (0, 2, 1, 3, 4))
    return rolled.reshape(caps_count * comps * shifts.shape[1], lat_count * lon_count)


def contract(left, right):
    return lax.dot_general(
        left, right, (((1,), (1,)), ((), ())), preferred_element_type=jnp.float32
    )


def per_device(positions, densities, operator, target_shift, weights):
    source = jnp.concatenate([positions, densities], axis=1)
    caps_here = source.shape[0]
    targets = target_shift.shape[1]
    rows = shifted_rows(source, target_shift)
    piece = lax.all_gather(operator, "cell", axis=0, tiled=True)
    rotated = contract(rows, piece.reshape(piece.shape[0], -1))
    partial_value = rotated.reshape(caps_here, 6, targets, -1)
    summed = lax.psum(partial_value, "band")
    velocity = stokes(summed[:, 0:3, :, 0], summed, weights)
    return velocity


def solution(mesh):
    in_specs = (
        P("cell", None, "band", None),
        P("cell", None, "band", None),
        P("cell", "band", None),
        P("cell", None),
        P(),
    )
    out_specs = P("cell", None, None)
    return jax.shard_map(
        per_device, mesh=mesh, in_specs=in_specs, out_specs=out_specs, check_vma=False
    )
```

profile of v0, /device:TPU:0, one launch (start us, length us, event | category | flops | bytes accessed | tf_op | source)
XLA Modules:
  0.0 182.1 jit_solution(361846499358096142)
XLA Ops:
  6.5 0.0 copy-start.1
  6.5 0.0 all-gather.2.cloned.1.call-start
  6.5 2.5 %copy.14 = bf16[40,48,192]{2,0,1:T(8,128)(2,1)} copy(bf16[40,48,192]{2,1,0:T(8,128)(2,1)} %param.7) | data formatting | bytes 1474560 | tf_op args[2]
  9.1 0.0 all-gather.2.cloned.1.call-update
  9.1 0.0 all-reduce.3.cloned.1.call-start
  9.1 1.3 maximum_maximum_fusion
  10.4 1.2 copy.12
  11.7 0.0 copy-done.1
  11.7 0.1 reshape.15
  11.8 8.6 %gather_fusion = bf16[32,6,48,192]{2,1,3,0:T(8,128)(2,1)} fusion(bf16[2,6,48,384]{2,1,0,3:T(8,128)(2,1)S(1)} %copy.12, s32[32]{0:T(128)S(1)} %reshape.15), kind=kCustom, calls=%fused_computation | custom fusion | bytes 7078400 | tf_op jit(solution)/shard_map/vmap(vmap())/gather | solution.py:28
  20.4 14.0 %copy.13 = bf16[2,16,6,48,192]{4,1,3,2,0:T(8,128)(2,1)} copy(bf16[2,16,6,48,192]{3,2,4,1,0:T(8,128)(2,1)} %bitcast.23) | data formatting | bytes 7077888 | tf_op jit(solution)/shard_map/vmap(vmap())/gather | solution.py:28
  34.4 0.0 copy-start
  34.4 97.8 %all-gather.2.cloned.1.call-done = bf16[640,48,192]{2,0,1:T(8,128)(2,1)} async-done(((bf16[40,48,192]{2,0,1:T(8,128)(2,1)}), bf16[640,48,192]{2,0,1:T(8,128)(2,1)}) %all-gather.2.cloned.1.call-update) | async-done | bytes 11796496 | tf_op jit(solution)/shard_map/all_gather | solution.py:48
  132.2 12.8 %fusion.3 = f32[2,6,16,640]{3,2,1,0:T(8,128)} fusion(bf16[640,48,192]{2,0,1:T(8,128)(2,1)} %all-gather.2.cloned.1.call-done, bf16[2,16,6,48,192]{4,1,3,2,0:T(8,128)(2,1)} %copy.13), kind=kOutput, calls=%fused_computation.4 | convolution fusion | flops 2264924160 | bytes 15826944 | tf_op jit(solution)/shard_map/dot_general | solution.py:38
  145.0 0.0 all-reduce.3.cloned.1.call-update
  145.0 26.2 %all-reduce.3.cloned.1.call-done = f32[2,6,16,640]{3,2,1,0:T(8,128)} async-done(((f32[2,6,16,640]{3,2,1,0:T(8,128)}), f32[2,6,16,640]{3,2,1,0:T(8,128)}) %all-reduce.3.cloned.1.call-update) | async-done | bytes 491536 | tf_op jit(solution)/shard_map/psum | solution.py:51
  171.2 0.8 slice.19
  172.0 0.1 copy.15
  172.1 1.2 multiply_reduce_fusion.1
  173.3 0.0 copy-done
  173.4 1.3 multiply_reduce_fusion
  174.7 0.6 copy.17
  (3 shorter events, 0.1 us)
Async XLA Ops:
  6.5 5.1 %copy-start.1 = (s32[2,16]{1,0:T(2,128)S(1)}, s32[2,16]{1,0:T(2,128)}, u32[]{:S(2)}) copy-start(s32[2,16]{1,0:T(2,128)} %param.8) | copy-start | bytes 388
  6.5 125.7 %all-gather.2.cloned.1.call-start = ((), (), s32[]{:S(2)}) async-start(), calls=%async_computation | async-start | bytes 16711680 | tf_op jit(solution)/shard_map/all_gather | solution.py:48
  9.1 162.2 %all-reduce.3.cloned.1.call-start = ((), (), s32[]{:S(2)}) async-start(), calls=%async_computation.1 | async-start | bytes 983040 | tf_op jit(solution)/shard_map/psum | solution.py:51
  34.4 139.0 %copy-start = (f32[640]{0:T(1024)S(1)}, f32[640]{0:T(1024)}, u32[]{:S(2)}) copy-start(f32[640]{0:T(1024)} %param.9) | copy-start | bytes 7684
Sparse Core Ops, SparseCore 0:
  9.7 122.4 all-gather.1
  145.2 26.0 all-reduce.2
where the time goes:
time: 182 us
  waiting for transfers between devices  124 us (68%)
  local copies, waits for them, and re-layouts  27.9 us (15%)
  between operations  13.5 us (7%)
  matrix products  12.8 us (7%)
  other arithmetic  3.8 us (2%)
    all_gather x1, waiting for transfers between devices, per_device(): piece = lax.all_gather(operator, 'cell', axis=0, tiled=True)  97.8 us
    psum x1, waiting for transfers between devices, per_device(): summed = lax.psum(partial_value, 'band')  26.2 us
    gather x3, local copies, waits for them, and re-layouts, per_target(): lax.dynamic_slice(block, (zero, zero, offset), (comps, lat_count, lon_cou...  22.7 us
    dot_general x1, matrix products, contract(): lax.dot_general(left, right, (((1,), (1,)), ((), ())), preferred_element_...  12.8 us
  transfers between devices with their start and end apart: 2, of which 2 were waited for; matrix products, arithmetic and copies ran while one was open for 14% of the time, Pallas kernels for 0%

commit v1 on v0

--- a/solution.py
+++ b/solution.py
@@ -48,7 +48,7 @@
     piece = lax.all_gather(operator, "cell", axis=0, tiled=True)
     rotated = contract(rows, piece.reshape(piece.shape[0], -1))
     partial_value = rotated.reshape(caps_here, 6, targets, -1)
-    summed = lax.psum(partial_value, "band")
+    summed = lax.all_gather(partial_value, "band").sum(axis=0)
     velocity = stokes(summed[:, 0:3, :, 0], summed, weights)
     return velocity
 

time: 182 us -> 167 us (0.918)
  waiting for transfers between devices: 124 us -> 97.9 us
  blocking collectives: 0 us -> 14 us
  other arithmetic: 3.8 us -> 1.75 us
    psum x1 -> x0, waiting for transfers between devices: 26.2 us -> none  [per_device(): summed = lax.psum(partial_value, 'band')]
    all_gather x0 -> x1, blocking collectives: none -> 14 us  [per_device(): summed = lax.all_gather(partial_value, 'band').sum(axis=0)]
  transfers between devices with their start and end apart: 2 -> 1, of which waited for: 2 -> 1; matrix products, arithmetic and copies ran while one was open for 14% -> 15% of each run, Pallas kernels for 0% -> 0%
where the time goes in v1:
time: 167 us; the launch traced here: 166 us
  waiting for transfers between devices  97.9 us (59%)
  local copies, waits for them, and re-layouts  27.1 us (16%)
  blocking collectives  14 us (8%)
  between operations  13.5 us (8%)
  matrix products  12 us (7%)
  other arithmetic  1.75 us (1%)
    all_gather x1, waiting for transfers between devices, per_device(): piece = lax.all_gather(operator, 'cell', axis=0, tiled=True)  97.9 us
    gather x3, local copies, waits for them, and re-layouts, per_target(): lax.dynamic_slice(block, (zero, zero, offset), (comps, lat_count, lon_cou...  22.7 us
    all_gather x1, blocking collectives, per_device(): summed = lax.all_gather(partial_value, 'band').sum(axis=0)  14 us
    dot_general x1, matrix products, contract(): lax.dot_general(left, right, (((1,), (1,)), ((), ())), preferred_element_...  12 us
  transfers between devices with their start and end apart: 1, of which 1 were waited for; matrix products, arithmetic and copies ran while one was open for 15% of the time, Pallas kernels for 0%

profile of v1, /device:TPU:0, one launch (start us, length us, event | category | flops | bytes accessed | tf_op | source)
XLA Modules:
  0.0 166.3 jit_solution(16971250420751647041)
XLA Ops:
  6.5 0.0 copy-start.1
  6.5 0.0 all-gather.3.cloned.1.call-start
  6.5 2.5 %copy.17 = bf16[40,48,192]{2,0,1:T(8,128)(2,1)} copy(bf16[40,48,192]{2,1,0:T(8,128)(2,1)} %param.7) | data formatting | bytes 1474560 | tf_op args[2]
  9.1 0.0 all-gather.3.cloned.1.call-update
  9.1 1.3 maximum_maximum_fusion
  10.4 1.2 copy.15
  11.6 0.0 copy-done.1
  11.6 0.1 reshape.17
  11.7 8.6 %gather_fusion = bf16[32,6,48,192]{2,1,3,0:T(8,128)(2,1)} fusion(bf16[2,6,48,384]{2,1,0,3:T(8,128)(2,1)S(1)} %copy.15, s32[32]{0:T(128)S(1)} %reshape.17), kind=kCustom, calls=%fused_computation | custom fusion | bytes 7078400 | tf_op jit(solution)/shard_map/vmap(vmap())/gather | solution.py:28
  20.3 14.0 %copy.16 = bf16[2,16,6,48,192]{4,1,3,2,0:T(8,128)(2,1)} copy(bf16[2,16,6,48,192]{3,2,4,1,0:T(8,128)(2,1)} %bitcast.24) | data formatting | bytes 7077888 | tf_op jit(solution)/shard_map/vmap(vmap())/gather | solution.py:28
  34.3 0.0 copy-start
  34.3 97.9 %all-gather.3.cloned.1.call-done = bf16[640,48,192]{2,0,1:T(8,128)(2,1)} async-done(((bf16[40,48,192]{2,0,1:T(8,128)(2,1)}), bf16[640,48,192]{2,0,1:T(8,128)(2,1)}) %all-gather.3.cloned.1.call-update) | async-done | bytes 11796496 | tf_op jit(solution)/shard_map/all_gather | solution.py:48
  132.2 12.0 %fusion.3 = f32[2,6,16,640]{3,2,1,0:T(8,128)S(1)} fusion(bf16[640,48,192]{2,0,1:T(8,128)(2,1)} %all-gather.3.cloned.1.call-done, bf16[2,16,6,48,192]{4,1,3,2,0:T(8,128)(2,1)} %copy.16), kind=kOutput, calls=%fused_computation.4 | convolution fusion | flops 2264924160 | bytes 15826944 | tf_op jit(solution)/shard_map/dot_general | solution.py:38
  144.2 14.0 %all-gather = f32[4,6,16,640]{3,2,1,0:T(8,128)S(1)} all-gather(f32[2,6,16,640]{3,2,1,0:T(8,128)S(1)} %fusion.3), channel_id=2, replica_groups=mesh['cell'=16,'band'=2] {'band'}, dimensions={0}, use_global_device_ids=true | all-gather | bytes 1474560 | tf_op jit(solution)/shard_map/all_gather | solution.py:51
  158.3 0.1 reduce_sum.36
  158.4 0.1 copy.18
  158.5 0.1 multiply_reduce_fusion.1
  158.6 0.0 copy-done
  158.7 0.2 multiply_reduce_fusion
  158.9 0.6 copy.20
  (4 shorter events, 0.1 us)
Async XLA Ops:
  6.5 5.1 %copy-start.1 = (s32[2,16]{1,0:T(2,128)S(1)}, s32[2,16]{1,0:T(2,128)}, u32[]{:S(2)}) copy-start(s32[2,16]{1,0:T(2,128)} %param.8) | copy-start | bytes 388
  6.5 125.7 %all-gather.3.cloned.1.call-start = ((), (), s32[]{:S(2)}) async-start(), calls=%async_computation | async-start | bytes 16711680 | tf_op jit(solution)/shard_map/all_gather | solution.py:48
  34.3 124.3 %copy-start = (f32[640]{0:T(1024)S(1)}, f32[640]{0:T(1024)}, u32[]{:S(2)}) copy-start(f32[640]{0:T(1024)} %param.9) | copy-start | bytes 7684
Sparse Core Ops, SparseCore 0:
  9.7 122.4 all-gather.2
